TPU v7x, 512 devices: a 8x2x16 block of a 8x8x16 slice. The times are simulated.
512 devices in a mesh: grp: 2 (over y), tp: 128 (over x, z), sub: 2 (over core).
Axes of the slice: x: 8, y: 2, z: 16, core: 2. Of those that a mesh axis runs over, the one named last changes fastest.
The devices are a block of a 8x8x16 slice.
Arguments:
- hidden_in: bfloat16 [32, 2, 4096], P('grp', 'sub', 'tp'), parts along dimension 0, may hold values from -16 to 16
- norm_attn: float32 [8192], replicated, may hold values from 0.25 to 1.75
- w_query: bfloat16 [8192, 2, 4096], P(None, 'sub', 'tp'), may hold values from -0.0625 to 0.0625
- w_key: bfloat16 [8192, 2, 512], P(None, 'sub', 'tp'), may hold values from -0.0625 to 0.0625
- w_value: bfloat16 [8192, 2, 512], P(None, 'sub', 'tp'), may hold values from -0.0625 to 0.0625
- w_out: bfloat16 [2, 4096, 2, 4096], P('sub', None, None, 'tp'), may hold values from -0.0625 to 0.0625
- norm_ffn: float32 [8192], replicated, may hold values from 0.25 to 1.75
- w_gate: bfloat16 [2, 4096, 14336], P('sub', None, 'tp'), may hold values from -0.0625 to 0.0625
- w_up: bfloat16 [2, 4096, 14336], P('sub', None, 'tp'), may hold values from -0.0625 to 0.0625
- w_down: bfloat16 [14336, 2, 4096], P('tp', 'sub'), may hold values from -0.1875 to 0.1875
- cache_keys: bfloat16 [32, 1024, 8, 128], P('grp', 'tp', 'sub'), parts along dimension 0, may hold values from -250 to 250
- cache_values: bfloat16 [32, 1024, 8, 128], P('grp', 'tp', 'sub'), parts along dimension 0, may hold values from -6 to 6
- lengths: int32 [32], P('grp'), parts along dimension 0, may hold values from 1 to 1024, as said below
Outputs:
- hidden_out: bfloat16 [32, 2, 4096], P('grp', 'sub', 'tp'), parts along dimension 0
There are 2 independent parts, one for each index of `grp`. A program takes and returns all parts, laid end to end along the dimension named above; an argument that names none is the same for every part. Nothing has to cross between parts.
Inputs may be any that keep to these rules, and one draw needn't show every extreme that they name: `lengths`: some sequence has 1024 live positions and some has 1.
All inputs are finite; a program needn't handle non-finite values.
Results may differ from a plain program's by a relative error of at most 0.012.
The roundings to bfloat16 on the way count: a program that leaves them out, or rounds other values in their place, can miss the bound.
Values may be sent and summed in bfloat16 or wider, within the bound.
A program may use at most 128 MiB of HBM per device.

v0:
```python
import math
import jax
import jax.numpy as jnp
from jax import lax
from jax.sharding import Mesh
from jax.sharding import PartitionSpec as P

HD = 128
TP = ("tp_0", "tp_1")
epsilon = 1e-05
rope_base = 500000.0
floor_score = -1e30


def joined_along(parts, dim):
    shape = list(parts.shape[1:])
    shape[dim] *= parts.shape[0]
    return jnp.moveaxis(parts, 0, dim).reshape(shape)


def gather_in_order(array, axes, sequence):
    parts = array[None]
    for k in sequence:
        parts = lax.all_gather(parts, axes[k], axis=0, tiled=True)
    carried = [lax.axis_size(axes[k]) for k in reversed(sequence)]
    parts = parts.reshape(*carried, *array.shape)
    turned = sorted(range(len(sequence)), key=lambda place: sequence[len(sequence) - 1 - place])
    return parts.transpose(*turned, *range(len(sequence), parts.ndim)).reshape(-1, *array.shape)


def whole_of(array, axes, sequence, dim):
    return joined_along(gather_in_order(array, axes, sequence), dim)


def sent_to_all(array, axis):
    copies = jnp.broadcast_to(array, (lax.axis_size(axis), *array.shape))
    return lax.all_to_all(copies, axis, split_axis=0, concat_axis=0, tiled=True)


def gathered_copies(array, axis, dim):
    parts = sent_to_all(array, axis)
    return joined_along(parts, dim)


def side_by_side(arrays, axis, dim, along):
    both = jnp.concatenate(arrays, axis=along)
    filled, at, gathered = (lax.all_gather(both, axis, axis=dim, tiled=True), 0, [])
    for a in arrays:
        gathered.append(lax.slice_in_dim(filled, at, at + a.shape[along], axis=along))
        at += a.shape[along]
    return tuple(gathered)


def collected_together(array, axis):
    leaves = jax.tree.leaves(array)
    sequence = sorted(range(len(leaves)), key=lambda k: -leaves[k].size)
    width = (1, *leaves[sequence[0]].shape)[-1]
    lines = [
        jnp.pad(leaves[k].reshape(-1), (0, -leaves[k].size % width)).reshape(-1, width)
        for k in sequence
    ]
    both, at, found = (lax.all_gather(jnp.concatenate(lines), axis), 0, {})
    for k, line in zip(sequence, lines):
        section = both[:, at : at + len(line)].reshape(len(both), -1)
        found[k] = section[:, : leaves[k].size].reshape(-1, *leaves[k].shape)
        at += len(line)
    numbers = iter(range(len(leaves)))
    return jax.tree.map(lambda _: found[next(numbers)], array)


def combined_by_axis(array, axes, combine):
    for axis in axes:
        pieces = collected_together(array, axis)
        array = jax.tree.map(lambda part: part[0], pieces)
        for k in range(1, lax.axis_size(axis)):
            array = combine(array, jax.tree.map(lambda part: part[k], pieces))
    return array


def cut_along(array, dim, size):
    shape = array.shape
    parts = array.reshape(*shape[:dim], size, shape[dim] // size, *shape[dim + 1 :])
    return jnp.moveaxis(parts, dim, 0)


def sum_at_owner(array, axis, dim):
    parts = cut_along(array, dim, lax.axis_size(axis))
    arrived = lax.all_to_all(parts, axis, split_axis=0, concat_axis=0, tiled=True)
    return arrived.sum(axis=0)


def over_pieces(array, axis):
    return lax.all_gather(array, axis).sum(0)


def over_copies(array, axis):
    return sent_to_all(array, axis).sum(axis=0)


def in_one(arrays, axis):
    vector, at, gathered = (jnp.concatenate([a.reshape(-1) for a in arrays]), 0, [])
    so_far = over_copies(vector, axis)
    for a in arrays:
        gathered.append(so_far[at : at + a.size].reshape(a.shape))
        at += a.size
    return tuple(gathered)


def summed_rows(array, axes, dim):
    for axis in axes:
        array = lax.psum_scatter(array, axis, scatter_dimension=dim, tiled=True)
    return array


def rope_angles(lengths):
    frequencies = rope_base ** (-(jnp.arange(HD // 2, dtype=jnp.float32) * 2.0) / HD)
    return lengths.astype(jnp.float32)[:, None] * frequencies[None, :]


def rotate(vectors, angles):
    middle_index = vectors.shape[-1] // 2
    cosine = jnp.cos(angles)[:, None, :]
    sine = jnp.sin(angles)[:, None, :]
    lower = vectors[..., :middle_index]
    upper = vectors[..., middle_index:]
    return jnp.concatenate([lower * cosine - upper * sine, upper * cosine + lower * sine], axis=-1)


def spread_rows(shard):
    across = whole_of(shard, TP, (0, 1), 2)
    return gathered_copies(across, "sub", 1)


def half_rows_of(shard):
    return whole_of(shard, TP, (0, 1), 2)


def join_partials(earlier, later):
    earlier_max, earlier_sum, earlier_out = earlier
    later_max, later_sum, later_out = later
    highest = jnp.maximum(earlier_max, later_max)
    earlier_scale = jnp.exp(earlier_max - highest)
    later_scale = jnp.exp(later_max - highest)
    joined_sum = earlier_sum * earlier_scale + later_sum * later_scale
    joined_out = earlier_out * earlier_scale[..., None] + later_out * later_scale[..., None]
    return (highest, joined_sum, joined_out)


def per_device(
    hidden_in,
    norm_attn,
    w_query,
    w_key,
    w_value,
    w_out,
    norm_ffn,
    w_gate,
    w_up,
    w_down,
    cache_keys,
    cache_values,
    lengths,
):
    seq_count = hidden_in.shape[0]
    shard_width = hidden_in.shape[2]
    half_width = shard_width * lax.axis_size(TP)
    model_width = half_width * lax.axis_size("sub")
    tp_pos = lax.axis_index(TP)
    sub_pos = lax.axis_index("sub")
    residual = hidden_in.astype(jnp.float32)
    whole_rows = spread_rows(hidden_in).astype(jnp.float32)
    factor = lax.rsqrt(jnp.mean(whole_rows * whole_rows, axis=(1, 2)) + epsilon)
    gain_whole = norm_attn.reshape(whole_rows.shape[1], half_width)
    gathered = (whole_rows * factor[:, None, None] * gain_whole).astype(jnp.bfloat16)
    flattened = gathered.reshape(seq_count, model_width)
    query_part = jnp.dot(
        flattened, w_query.reshape(model_width, -1), preferred_element_type=jnp.float32
    ).astype(jnp.bfloat16)
    key_part = jnp.dot(
        flattened, w_key.reshape(model_width, -1), preferred_element_type=jnp.float32
    ).astype(jnp.bfloat16)
    value_part = jnp.dot(
        flattened, w_value.reshape(model_width, -1), preferred_element_type=jnp.float32
    ).astype(jnp.bfloat16)
    query, key_new, value_new = (
        lax.all_gather(query_part, TP, axis=1, tiled=True),
        *side_by_side((key_part, value_part), TP, 1, 0),
    )
    query_heads = query.shape[1] // HD
    kv_heads = key_new.shape[1] // HD
    group_size = query_heads // kv_heads
    angles = rope_angles(lengths)
    query_rot = rotate(
        query.astype(jnp.float32).reshape(seq_count, query_heads, HD), angles
    ).astype(jnp.bfloat16)
    key_rot = rotate(key_new.astype(jnp.float32).reshape(seq_count, kv_heads, HD), angles).astype(
        jnp.bfloat16
    )
    grouped = query_rot.reshape(seq_count, kv_heads, group_size, HD)
    values_new = value_new.astype(jnp.float32).reshape(seq_count, kv_heads, 1, HD)
    span = cache_keys.shape[1]
    scores = jnp.einsum(
        "bkgd,blkd->bkgl", grouped, cache_keys, preferred_element_type=jnp.float32
    ) / math.sqrt(HD)
    places = tp_pos * span + jnp.arange(span, dtype=jnp.int32)
    live = (places[None, :] < lengths[:, None])[:, None, None, :]
    masked = jnp.where(live, scores, floor_score)
    local_max = jnp.max(masked, axis=-1)
    weights = jnp.where(live, jnp.exp(masked - local_max[..., None]), 0.0)
    local_sum = jnp.sum(weights, axis=-1)
    local_out = jnp.einsum(
        "bkgl,blkd->bkgd",
        weights,
        cache_values.astype(jnp.float32),
        precision=lax.Precision.HIGHEST,
    )
    own_score = jnp.sum(
        grouped.astype(jnp.float32) * key_rot.astype(jnp.float32)[:, :, None, :], axis=-1
    ) / math.sqrt(HD)
    joined_max, joined_sum, joined_out = combined_by_axis(
        (local_max, local_sum, local_out), TP, join_partials
    )
    highest = jnp.maximum(joined_max, own_score)
    kept_scale = jnp.exp(joined_max - highest)
    own_weight = jnp.exp(own_score - highest)
    numerator = joined_out * kept_scale[..., None] + own_weight[..., None] * values_new
    denominator = joined_sum * kept_scale + own_weight
    attended = (numerator / denominator[..., None]).reshape(seq_count, -1).astype(jnp.bfloat16)
    out_part = jnp.dot(
        attended, w_out.reshape(attended.shape[1], -1), preferred_element_type=jnp.float32
    )
    out_part = out_part.reshape(seq_count, -1, shard_width)
    mixed = sum_at_owner(out_part, "sub", 1)
    middle = (residual + mixed).astype(jnp.bfloat16)
    middle_float = middle.astype(jnp.float32)
    raw_half = half_rows_of(middle).astype(jnp.float32)
    partial_squares = jnp.sum(raw_half * raw_half, axis=(1, 2))
    squares_mid = over_pieces(partial_squares, "sub")
    factor_mid = lax.rsqrt(squares_mid / model_width + epsilon)
    gain_half = lax.dynamic_slice_in_dim(norm_ffn, sub_pos * half_width, half_width)
    half_rows = (raw_half * factor_mid[:, None, None] * gain_half).astype(jnp.bfloat16)
    half_flat = half_rows.reshape(seq_count, half_width)
    gate_part = jnp.dot(
        half_flat, w_gate.reshape(half_width, -1), preferred_element_type=jnp.float32
    )
    up_part = jnp.dot(half_flat, w_up.reshape(half_width, -1), preferred_element_type=jnp.float32)
    gate_total, up_total = in_one((gate_part, up_part), "sub")
    hidden = (jax.nn.silu(gate_total) * up_total).astype(jnp.bfloat16)
    down_part = jnp.dot(
        hidden, w_down.reshape(hidden.shape[1], -1), preferred_element_type=jnp.float32
    )
    down_share = summed_rows(down_part, TP, 1)
    return (middle_float + down_share[:, None, :]).astype(jnp.bfloat16)


def solution(mesh):
    split = Mesh(
        mesh.devices.reshape(mesh.shape["grp"], 8, 16, mesh.shape["sub"]),
        ("grp", "tp_0", "tp_1", "sub"),
    )
    return jax.shard_map(
        per_device,
        mesh=split,
        in_specs=(
            P("grp", "sub", TP),
            P(),
            P(None, "sub", TP),
            P(None, "sub", TP),
            P(None, "sub", TP),
            P("sub", None, None, TP),
            P(),
            P("sub", None, TP),
            P("sub", None, TP),
            P(TP, "sub", None),
            P("grp", TP, "sub", None),
            P("grp", TP, "sub", None),
            P("grp"),
        ),
        out_specs=P("grp", "sub", TP),
        check_vma=False,
    )
```

profile of v0, /device:TPU:66, one launch (start us, length us, event | category | flops | bytes accessed | tf_op | source)
XLA Modules:
  0.0 595.9 jit_solution(17651004225491951101)
XLA Ops:
  6.6 62.3 %all-gather = bf16[128,1,32]{2,0,1:T(8,128)(2,1)S(1)} all-gather(bf16[16,1,32]{2,0,1:T(8,128)(2,1)} %param.13), channel_id=2, replica_groups=mesh['grp'=2,'tp_0'=8,'tp_1'=16,'sub'=2] {'tp_0'}, dimensions={0}, use_global_device_ids=true | all-gather | bytes 9216 | tf_op jit(solution)/shard_map/all_gather | solution.py:24
  68.8 34.6 %all_gather.37 = bf16[128,16,1,32]{3,1,2,0:T(8,128)(2,1)S(1)} all-gather(bf16[8,16,1,32]{3,1,2,0:T(8,128)(2,1)S(1)} %bitcast.547), channel_id=1, replica_groups=mesh['grp'=2,'tp_0'=8,'tp_1'=16,'sub'=2] {'tp_1'}, dimensions={0}, use_global_device_ids=true | all-gather | bytes 139264 | tf_op jit(solution)/shard_map/all_gather | solution.py:24
  104.1 0.7 broadcast_in_dim.30
  104.9 3.5 all-to-all-start
  108.6 1.3 all-to-all-done
  110.9 87.2 %all-gather.5 = bf16[128,32,16]{1,2,0:T(8,128)(2,1)S(1)} all-gather(bf16[1,32,16]{1,2,0:T(8,128)(2,1)S(1)} %fusion.1), channel_id=1, replica_groups=mesh['grp'=2,'tp_0'=8,'tp_1'=16,'sub'=2] {'tp_0','tp_1'}, dimensions={0}, use_global_device_ids=true | all-gather | bytes 132096 | tf_op jit(solution)/shard_map/all_gather | solution.py:186
  201.9 39.4 %all-gather.10.cloned.1.call-done = f32[4160,128]{1,0:T(8,128)} async-done(((f32[520,128]{1,0:T(8,128)}), f32[4160,128]{1,0:T(8,128)}) %all-gather.10.cloned.1.call-update) | async-done | bytes 2129936 | tf_op jit(solution)/shard_map/all_gather | solution.py:62
  241.3 0.8 fusion.56
  244.9 2.5 fusion.16
  247.4 0.7 pad_maximum_fusion.1
  248.9 89.8 %all-gather.6 = bf16[128,4,32]{2,1,0:T(4,128)(2,1)S(1)} all-gather(bf16[1,4,32]{2,1,0:T(4,128)(2,1)S(1)} %maximum_bitcast_fusion), channel_id=1, replica_groups=mesh['grp'=2,'tp_0'=8,'tp_1'=16,'sub'=2] {'tp_0','tp_1'}, dimensions={0}, use_global_device_ids=true | all-gather | bytes 33024 | tf_op jit(solution)/shard_map/all_gather | solution.py:47
  339.5 1.3 dynamic-slice
  341.6 0.9 multiply_reduce_fusion
  342.5 1.4 fusion.109
  343.9 1.5 fusion.108
  345.4 3.5 fusion.110
  348.8 1.4 squeeze.268
  350.2 1.4 squeeze.288
  351.6 1.4 squeeze.286
  353.0 1.4 squeeze.284
  354.3 1.4 squeeze.282
  355.7 1.4 squeeze.280
  357.1 1.4 squeeze.278
  358.5 1.4 squeeze.276
  359.9 1.4 squeeze.274
  361.2 1.4 squeeze.272
  362.6 1.4 squeeze.270
  364.0 1.3 squeeze.266
  365.3 1.4 squeeze.265
  366.7 1.4 squeeze.294
  368.1 1.4 squeeze.292
  369.5 1.4 squeeze.290
  370.9 1.4 squeeze.311
  372.2 1.4 squeeze.310
  373.6 1.4 squeeze.309
  375.0 1.4 squeeze.308
  376.4 1.4 squeeze.307
  377.7 1.4 squeeze.306
  379.1 1.4 squeeze.305
  380.5 1.4 squeeze.304
  381.9 1.4 squeeze.303
  383.3 1.4 squeeze.302
  384.7 1.4 squeeze.301
  386.0 1.4 squeeze.300
  387.4 1.4 squeeze.299
  388.8 1.4 squeeze.298
  390.2 1.4 squeeze.297
  391.6 1.4 squeeze.296
  393.0 1.1 maximum_maximum_fusion
  394.1 1.7 multiply_add_fusion
  395.9 3.3 divide_convert_fusion
  399.2 1.0 reshape.2406
  400.2 1.5 fusion.113
  401.7 3.7 all_to_all.16
  407.4 24.7 %all-gather.3 = bf16[128,1,32]{2,0,1:T(8,128)(2,1)S(1)} all-gather(bf16[16,1,32]{2,0,1:T(8,128)(2,1)S(1)} %fusion.51), channel_id=5, replica_groups=mesh['grp'=2,'tp_0'=8,'tp_1'=16,'sub'=2] {'tp_0'}, dimensions={0}, use_global_device_ids=true | all-gather | bytes 9216 | tf_op jit(solution)/shard_map/all_gather | solution.py:24
  432.2 30.3 %all_gather.45 = bf16[128,16,1,32]{3,1,2,0:T(8,128)(2,1)S(1)} all-gather(bf16[8,16,1,32]{3,1,2,0:T(8,128)(2,1)S(1)} %bitcast.548), channel_id=1, replica_groups=mesh['grp'=2,'tp_0'=8,'tp_1'=16,'sub'=2] {'tp_1'}, dimensions={0}, use_global_device_ids=true | all-gather | bytes 139264 | tf_op jit(solution)/shard_map/all_gather | solution.py:24
  463.1 2.5 all-reduce
  467.4 1.6 fusion.7
  469.2 3.8 all_to_all.17
  473.1 1.0 fusion.3
  474.2 39.7 %reduce-scatter.5.cloned.1.call-done = f32[16,512]{1,0:T(8,128)} async-done(((f32[16,4096]{1,0:T(8,128)}), f32[16,512]{1,0:T(8,128)}) %reduce-scatter.5.cloned.1.call-update) | async-done | bytes 32784 | tf_op jit(solution)/shard_map/reduce_scatter | solution.py:111
  514.0 1.6 copy.106
  515.6 72.4 %reduce-scatter.7.cloned.1.call-done = f32[32,16]{1,0:T(8,128)} async-done(((f32[512,16]{1,0:T(8,128)}), f32[32,16]{1,0:T(8,128)}) %reduce-scatter.7.cloned.1.call-update) | async-done | bytes 2064
  588.0 0.8 copy.107
  (109 shorter events, 15.7 us)
Async XLA Ops:
  6.5 466.6 %copy-start = (bf16[112,1,4096]{2,0,1:T(8,128)(2,1)S(1)}, bf16[112,1,4096]{2,0,1:T(8,128)(2,1)}, u32[]{:S(2)}) copy-start(bf16[112,1,4096]{2,0,1:T(8,128)(2,1)} %param.22) | copy-start | bytes 2752516
  68.8 39.6 %copy-start.14 = (s32[16]{0:T(128)S(1)}, s32[16]{0:T(128)}, u32[]{:S(2)}) copy-start(s32[16]{0:T(128)} %param.25) | copy-start | bytes 196
  68.8 39.7 %copy-start.12 = (f32[8192]{0:T(1024)S(1)}, f32[8192]{0:T(1024)}, u32[]{:S(2)}) copy-start(f32[8192]{0:T(1024)} %param.14) | copy-start | bytes 98308
  103.4 7.2 %copy-start.8 = (bf16[8192,1,32]{0,2,1:T(8,128)(2,1)S(1)}, bf16[8192,1,32]{0,2,1:T(8,128)(2,1)}, u32[]{:S(2)}) copy-start(bf16[8192,1,32]{0,2,1:T(8,128)(2,1)} %param.15) | copy-start | bytes 1572868
  104.9 5.0 all-to-all-start
  108.3 132.9 %all-gather.10.cloned.1.call-start = ((), (), s32[]{:S(2)}) async-start(), calls=%async_computation.6 | async-start | bytes 2396160 | tf_op jit(solution)/shard_map/all_gather | solution.py:62
  198.1 1.6 copy-start.10
  198.9 1.5 copy-start.11
  200.9 47.5 %copy-start.15 = (bf16[8192,1,4]{0,2,1:T(4,128)(2,1)S(1)}, bf16[8192,1,4]{0,2,1:T(4,128)(2,1)}, u32[]{:S(2)}) copy-start(bf16[8192,1,4]{0,2,1:T(4,128)(2,1)} %param.17) | copy-start | bytes 196612
  201.0 47.6 %copy-start.16 = (bf16[8192,1,4]{0,2,1:T(4,128)(2,1)S(1)}, bf16[8192,1,4]{0,2,1:T(4,128)(2,1)}, u32[]{:S(2)}) copy-start(bf16[8192,1,4]{0,2,1:T(4,128)(2,1)} %param.16) | copy-start | bytes 196612
  201.8 140.7 %all-gather.12.cloned.1.call-start = ((), (), s32[]{:S(2)}) async-start(), calls=%async_computation.7 | async-start | bytes 4526080 | tf_op jit(solution)/shard_map/all_gather | solution.py:62
  244.9 96.5 %copy-start.13 = (f32[8192]{0:T(1024)S(1)}, f32[8192]{0:T(1024)}, u32[]{:S(2)}) copy-start(f32[8192]{0:T(1024)} %param.19) | copy-start | bytes 98308
  248.2 265.8 %reduce-scatter.5.cloned.1.call-start = ((), (), s32[]{:S(2)}) async-start(), calls=%async_computation.5 | async-start | bytes 294912 | tf_op jit(solution)/shard_map/reduce_scatter | solution.py:111
  392.9 2.9 copy-start.1
  392.9 2.9 copy-start.2
  392.9 2.9 copy-start.3
  392.9 3.0 copy-start.4
  392.9 3.0 copy-start.5
  393.0 3.0 copy-start.6
  393.0 3.0 copy-start.9
  465.8 1.2 copy-start.7
  474.1 113.9 %reduce-scatter.7.cloned.1.call-start = ((), (), s32[]{:S(2)}) async-start(), calls=%async_computation.8 | async-start | bytes 278528
Sparse Core Ops, SparseCore 0:
  201.9 39.2 all-gather.9
  248.3 79.5 all-gather.11
  474.3 39.6 reduce-scatter.4
  516.6 71.3 reduce-scatter.6
where the time goes:
time: 598 us; the launch traced here: 596 us
  blocking collectives  339 us (57%)
  waiting for transfers between devices  153 us (26%)
  local copies, waits for them, and re-layouts  61.8 us (10%)
  other arithmetic  18.1 us (3%)
  between operations  14.3 us (2%)
    all_gather x4, blocking collectives, gather_in_order(): parts = lax.all_gather(parts, axes[k], axis=0, tiled=True)  152 us
    all_gather x1, blocking collectives, side_by_side(): lax.all_gather(both, axis, axis=dim, tiled=True)  89.8 us
    all_gather x1, blocking collectives, per_device(): lax.all_gather(query_part, TP, axis=1, tiled=True)  87.2 us
    unnamed x5, waiting for transfers between devices  72.6 us
    squeeze x30, local copies, waits for them, and re-layouts, combined_by_axis(): array = combine(array, jax.tree.map(lambda part: part[k], pieces))  41.3 us
    reduce_scatter x1, waiting for transfers between devices, summed_rows(): array = lax.psum_scatter(array, axis, scatter_dimension=dim, tiled=True)  39.7 us
    all_gather x2, waiting for transfers between devices, collected_together(): both, at, found = (lax.all_gather(jnp.concatenate(lines), axis), 0, {})  39.4 us
  transfers between devices with their start and end apart: 5, of which 4 were waited for; matrix products, arithmetic and copies ran while one was open for 1% of the time, Pallas kernels for 0%

commit v1 on v0

--- a/solution.py
+++ b/solution.py
@@ -10,6 +10,11 @@
 epsilon = 1e-05
 rope_base = 500000.0
 floor_score = -1e30
+
+
+def all_by_exchange(block, axis, dim):
+    sent = jnp.stack([block] * lax.axis_size(axis))
+    return jnp.concatenate(lax.all_to_all(sent, axis, 0, 0), axis=dim)
 
 
 def joined_along(parts, dim):
@@ -183,7 +188,7 @@
         flattened, w_value.reshape(model_width, -1), preferred_element_type=jnp.float32
     ).astype(jnp.bfloat16)
     query, key_new, value_new = (
-        lax.all_gather(query_part, TP, axis=1, tiled=True),
+        all_by_exchange(query_part, TP, 1),
         *side_by_side((key_part, value_part), TP, 1, 0),
     )
     query_heads = query.shape[1] // HD

time: 598 us -> 537 us (0.90)
  blocking collectives: 339 us -> 252 us
  waiting for transfers between devices: 153 us -> 167 us
  starting transfers between devices: 3.91 us -> 14.9 us
    all_gather x1 -> x0, blocking collectives: 87.2 us -> none  [per_device(): lax.all_gather(query_part, TP, axis=1, tiled=True)]
    all_to_all x0 -> x1, waiting for transfers between devices: none -> 17.4 us  [all_by_exchange(): return jnp.concatenate(lax.all_to_all(sent, axis, 0, 0), axis=dim)]
    all_to_all x0 -> x1, starting transfers between devices: none -> 11.1 us  [all_by_exchange(): return jnp.concatenate(lax.all_to_all(sent, axis, 0, 0), axis=dim)]
  transfers between devices with their start and end apart: 5 -> 6, of which waited for: 4 -> 5; matrix products, arithmetic and copies ran while one was open for 1% -> 1% of each run, Pallas kernels for 0% -> 0%
where the time goes in v1:
time: 537 us; the launch traced here: 535 us
  blocking collectives  252 us (47%)
  waiting for transfers between devices  167 us (31%)
  local copies, waits for them, and re-layouts  62.6 us (12%)
  other arithmetic  18.2 us (3%)
  starting transfers between devices  14.9 us (3%)
  between operations  14.4 us (3%)
  matrix products  5.95 us (1%)
    all_gather x4, blocking collectives, gather_in_order(): parts = lax.all_gather(parts, axes[k], axis=0, tiled=True)  152 us
    all_gather x1, blocking collectives, side_by_side(): lax.all_gather(both, axis, axis=dim, tiled=True)  90.1 us
    unnamed x5, waiting for transfers between devices  72.4 us
    squeeze x30, local copies, waits for them, and re-layouts, combined_by_axis(): array = combine(array, jax.tree.map(lambda part: part[k], pieces))  41.3 us
    reduce_scatter x1, waiting for transfers between devices, summed_rows(): array = lax.psum_scatter(array, axis, scatter_dimension=dim, tiled=True)  39.7 us
    all_gather x2, waiting for transfers between devices, collected_together(): both, at, found = (lax.all_gather(jnp.concatenate(lines), axis), 0, {})  36.3 us
    all_to_all x1, waiting for transfers between devices, all_by_exchange(): return jnp.concatenate(lax.all_to_all(sent, axis, 0, 0), axis=dim)  17.4 us
    all_to_all x1, starting transfers between devices, all_by_exchange(): return jnp.concatenate(lax.all_to_all(sent, axis, 0, 0), axis=dim)  11.1 us
  transfers between devices with their start and end apart: 6, of which 5 were waited for; matrix products, arithmetic and copies ran while one was open for 1% of the time, Pallas kernels for 0%

profile of v1, /device:TPU:66, one launch (start us, length us, event | category | flops | bytes accessed | tf_op | source)
XLA Modules:
  0.0 535.0 jit_solution(322187194634552637)
XLA Ops:
  6.6 62.3 %all-gather = bf16[128,1,32]{2,0,1:T(8,128)(2,1)S(1)} all-gather(bf16[16,1,32]{2,0,1:T(8,128)(2,1)} %param.13), channel_id=2, replica_groups=mesh['grp'=2,'tp_0'=8,'tp_1'=16,'sub'=2] {'tp_0'}, dimensions={0}, use_global_device_ids=true | all-gather | bytes 9216 | tf_op jit(solution)/shard_map/all_gather | solution.py:29
  68.8 34.4 %all_gather.34 = bf16[128,16,1,32]{3,1,2,0:T(8,128)(2,1)S(1)} all-gather(bf16[8,16,1,32]{3,1,2,0:T(8,128)(2,1)S(1)} %bitcast.538), channel_id=1, replica_groups=mesh['grp'=2,'tp_0'=8,'tp_1'=16,'sub'=2] {'tp_1'}, dimensions={0}, use_global_device_ids=true | all-gather | bytes 139264 | tf_op jit(solution)/shard_map/all_gather | solution.py:29
  104.7 3.5 all-to-all-start
  108.2 1.5 all-to-all-done
  110.8 1.0 reshape.2405
  111.9 11.1 %all-to-all-start.1 = ((bf16[128,2,256]{2,1,0:T(2,128)(2,1)}), bf16[128,2,256]{2,1,0:T(2,128)(2,1)S(1)}, u32[]{:S(2)}, u32[]{:S(2)}) async-start(bf16[128,2,256]{2,1,0:T(2,128)(2,1)} %reshape.2405), calls=%async_computation.1 | async-start | bytes 262144 | tf_op jit(solution)/shard_map/all_to_all | solution.py:17
  123.3 17.4 %all-to-all-done.1 = bf16[128,2,256]{2,1,0:T(2,128)(2,1)S(1)} async-done(((bf16[128,2,256]{2,1,0:T(2,128)(2,1)}), bf16[128,2,256]{2,1,0:T(2,128)(2,1)S(1)}, u32[]{:S(2)}, u32[]{:S(2)}) %all-to-all-start.1) | async-done | bytes 131104 | tf_op jit(solution)/shard_map/all_to_all | solution.py:17
  144.2 36.3 %all-gather.9.cloned.1.call-done = f32[4160,128]{1,0:T(8,128)} async-done(((f32[520,128]{1,0:T(8,128)}), f32[4160,128]{1,0:T(8,128)}) %all-gather.9.cloned.1.call-update) | async-done | bytes 2129936 | tf_op jit(solution)/shard_map/all_gather | solution.py:67
  180.5 0.8 fusion.55
  184.1 2.5 fusion.15
  188.0 90.1 %all-gather.5 = bf16[128,4,32]{2,1,0:T(4,128)(2,1)S(1)} all-gather(bf16[1,4,32]{2,1,0:T(4,128)(2,1)S(1)} %maximum_bitcast_fusion), channel_id=1, replica_groups=mesh['grp'=2,'tp_0'=8,'tp_1'=16,'sub'=2] {'tp_0','tp_1'}, dimensions={0}, use_global_device_ids=true | all-gather | bytes 33024 | tf_op jit(solution)/shard_map/all_gather | solution.py:52
  278.8 1.3 dynamic-slice
  280.9 0.9 multiply_reduce_fusion
  281.8 1.4 fusion.108
  283.2 1.5 fusion.107
  284.7 3.5 fusion.109
  288.2 1.4 squeeze.268
  289.6 1.3 squeeze.288
  290.9 1.4 squeeze.286
  292.3 1.4 squeeze.284
  293.7 1.4 squeeze.282
  295.0 1.4 squeeze.280
  296.4 1.4 squeeze.278
  297.8 1.4 squeeze.276
  299.2 1.4 squeeze.274
  300.5 1.4 squeeze.272
  301.9 1.4 squeeze.270
  303.3 1.4 squeeze.266
  304.7 1.4 squeeze.265
  306.1 1.4 squeeze.294
  307.5 1.3 squeeze.292
  308.8 1.4 squeeze.290
  310.2 1.4 squeeze.311
  311.5 1.4 squeeze.310
  312.9 1.4 squeeze.309
  314.3 1.4 squeeze.308
  315.7 1.4 squeeze.307
  317.0 1.4 squeeze.306
  318.4 1.4 squeeze.305
  319.8 1.4 squeeze.304
  321.2 1.4 squeeze.303
  322.6 1.4 squeeze.302
  324.0 1.4 squeeze.301
  325.3 1.4 squeeze.300
  326.7 1.4 squeeze.299
  328.1 1.4 squeeze.298
  329.5 1.4 squeeze.297
  330.9 1.4 squeeze.296
  332.3 1.1 maximum_maximum_fusion
  333.4 1.7 multiply_add_fusion
  335.3 3.3 divide_convert_fusion
  338.5 1.0 reshape.2400
  339.5 1.5 fusion.112
  341.1 3.7 all_to_all.21
  346.8 24.6 %all-gather.3 = bf16[128,1,32]{2,0,1:T(8,128)(2,1)S(1)} all-gather(bf16[16,1,32]{2,0,1:T(8,128)(2,1)S(1)} %fusion.50), channel_id=5, replica_groups=mesh['grp'=2,'tp_0'=8,'tp_1'=16,'sub'=2] {'tp_0'}, dimensions={0}, use_global_device_ids=true | all-gather | bytes 9216 | tf_op jit(solution)/shard_map/all_gather | solution.py:29
  371.4 30.3 %all_gather.41 = bf16[128,16,1,32]{3,1,2,0:T(8,128)(2,1)S(1)} all-gather(bf16[8,16,1,32]{3,1,2,0:T(8,128)(2,1)S(1)} %bitcast.539), channel_id=1, replica_groups=mesh['grp'=2,'tp_0'=8,'tp_1'=16,'sub'=2] {'tp_1'}, dimensions={0}, use_global_device_ids=true | all-gather | bytes 139264 | tf_op jit(solution)/shard_map/all_gather | solution.py:29
  402.4 2.5 all-reduce
  406.6 1.6 fusion.6
  408.4 3.8 all_to_all.22
  412.4 0.9 fusion.2
  413.5 39.7 %reduce-scatter.5.cloned.1.call-done = f32[16,512]{1,0:T(8,128)} async-done(((f32[16,4096]{1,0:T(8,128)}), f32[16,512]{1,0:T(8,128)}) %reduce-scatter.5.cloned.1.call-update) | async-done | bytes 32784 | tf_op jit(solution)/shard_map/reduce_scatter | solution.py:116
  453.1 1.6 copy.102
  454.8 72.2 %reduce-scatter.7.cloned.1.call-done = f32[32,16]{1,0:T(8,128)} async-done(((f32[512,16]{1,0:T(8,128)}), f32[32,16]{1,0:T(8,128)}) %reduce-scatter.7.cloned.1.call-update) | async-done | bytes 2064
  527.0 0.8 copy.103
  (112 shorter events, 16.9 us)
Async XLA Ops:
  6.5 405.9 %copy-start = (bf16[112,1,4096]{2,0,1:T(8,128)(2,1)S(1)}, bf16[112,1,4096]{2,0,1:T(8,128)(2,1)}, u32[]{:S(2)}) copy-start(bf16[112,1,4096]{2,0,1:T(8,128)(2,1)} %param.22) | copy-start | bytes 2752516
  6.6 101.6 %copy-start.12 = (f32[8192]{0:T(1024)S(1)}, f32[8192]{0:T(1024)}, u32[]{:S(2)}) copy-start(f32[8192]{0:T(1024)} %param.14) | copy-start | bytes 98308
  103.3 7.2 %copy-start.8 = (bf16[8192,1,32]{0,2,1:T(8,128)(2,1)S(1)}, bf16[8192,1,32]{0,2,1:T(8,128)(2,1)}, u32[]{:S(2)}) copy-start(bf16[8192,1,32]{0,2,1:T(8,128)(2,1)} %param.15) | copy-start | bytes 1572868
  104.7 5.0 all-to-all-start
  108.2 14.9 %copy-start.14 = (s32[16]{0:T(128)S(1)}, s32[16]{0:T(128)}, u32[]{:S(2)}) copy-start(s32[16]{0:T(128)} %param.25) | copy-start | bytes 196
  111.9 28.9 %all-to-all-start.1 = ((bf16[128,2,256]{2,1,0:T(2,128)(2,1)}), bf16[128,2,256]{2,1,0:T(2,128)(2,1)S(1)}, u32[]{:S(2)}, u32[]{:S(2)}) async-start(bf16[128,2,256]{2,1,0:T(2,128)(2,1)} %reshape.2405), calls=%async_computation.1 | async-start | bytes 262144 | tf_op jit(solution)/shard_map/all_to_all | solution.py:17
  123.0 57.5 %all-gather.9.cloned.1.call-start = ((), (), s32[]{:S(2)}) async-start(), calls=%async_computation.7 | async-start | bytes 2396160 | tf_op jit(solution)/shard_map/all_gather | solution.py:67
  141.1 0.9 copy-start.10
  141.1 1.5 copy-start.11
  143.2 44.3 %copy-start.15 = (bf16[8192,1,4]{0,2,1:T(4,128)(2,1)S(1)}, bf16[8192,1,4]{0,2,1:T(4,128)(2,1)}, u32[]{:S(2)}) copy-start(bf16[8192,1,4]{0,2,1:T(4,128)(2,1)} %param.17) | copy-start | bytes 196612
  143.3 44.4 %copy-start.16 = (bf16[8192,1,4]{0,2,1:T(4,128)(2,1)S(1)}, bf16[8192,1,4]{0,2,1:T(4,128)(2,1)}, u32[]{:S(2)}) copy-start(bf16[8192,1,4]{0,2,1:T(4,128)(2,1)} %param.16) | copy-start | bytes 196612
  144.1 137.7 %all-gather.11.cloned.1.call-start = ((), (), s32[]{:S(2)}) async-start(), calls=%async_computation.8 | async-start | bytes 4526080 | tf_op jit(solution)/shard_map/all_gather | solution.py:67
  184.1 96.6 %copy-start.13 = (f32[8192]{0:T(1024)S(1)}, f32[8192]{0:T(1024)}, u32[]{:S(2)}) copy-start(f32[8192]{0:T(1024)} %param.19) | copy-start | bytes 98308
  187.4 265.8 %reduce-scatter.5.cloned.1.call-start = ((), (), s32[]{:S(2)}) async-start(), calls=%async_computation.6 | async-start | bytes 294912 | tf_op jit(solution)/shard_map/reduce_scatter | solution.py:116
  332.3 2.9 copy-start.1
  332.3 2.9 copy-start.2
  332.3 2.9 copy-start.3
  332.3 3.0 copy-start.4
  332.3 3.0 copy-start.5
  332.3 3.0 copy-start.6
  332.3 3.0 copy-start.9
  405.1 1.2 copy-start.7
  413.4 113.6 %reduce-scatter.7.cloned.1.call-start = ((), (), s32[]{:S(2)}) async-start(), calls=%async_computation.9 | async-start | bytes 278528
Sparse Core Ops, SparseCore 0:
  144.2 36.1 all-gather.8
  187.5 79.5 all-gather.10
  413.5 39.5 reduce-scatter.4
  455.8 71.1 reduce-scatter.6
